TPU v7x, 32 devices: a whole 2x2x4 slice. The times are simulated.
32 devices in a mesh: row: 8 (over y, x, core), col: 4 (over z).
Axes of the slice: x: 2, y: 2, z: 4, core: 2. Of those that a mesh axis runs over, the one named last changes fastest.
Arguments:
- surface: bfloat16 [16384, 16384], P('row', 'col'), may hold values from -0.0234375 to 0.0234375
- excitation: float32 [16384, 128], P(('row', 'col')), may hold values from -6 to 6
- dtn_blocks: bfloat16 [32, 1024, 1024], P(('row', 'col')), may hold values from -0.09375 to 0.09375
- interp_blocks: bfloat16 [32, 1024, 2048], P(('row', 'col')), may hold values from -0.09375 to 0.09375
- adjacency: int32 [32, 6], P(('row', 'col')), may hold values from 0 to 31, as said below
Outputs:
- solution: float32 [16384, 128], P(('row', 'col'))
- residual: float32 [16384, 128], P(('row', 'col'))
Inputs may be any that keep to these rules, and one draw needn't show every extreme that they name: `adjacency`: entry [s, k] names a subdomain of the same spatial group as s (equal index // 4); it may name s itself, which adds nothing.
All inputs are finite; a program needn't handle non-finite values.
Results may differ from a plain program's by a relative error of at most 0.02.
Values may be sent and summed in bfloat16 or wider, within the bound.
A program may use at most 64 MiB of HBM per device.

v0:
```python
import jax
import jax.numpy as jnp
from jax import lax
from jax.sharding import PartitionSpec as P

ITERS = 2
NADJ = 6


damping = 0.25
face_weight = 0.25


def broadcast(value, axis, source):
    kept = jnp.where(lax.axis_index(axis) == source, value, 0).astype(value.dtype)
    return lax.psum(kept, axis)


def local(surface, excitation, dtn_blocks, interp_blocks, adjacency):
    col_count = lax.axis_size("col")
    row_count = lax.axis_size("row")
    col_index = lax.axis_index("col")
    dtn_block = dtn_blocks[0]
    interp_block = interp_blocks[0]
    local_adjacent = adjacency[0] % col_count
    current = excitation
    residual = excitation
    for sweep in range(ITERS):
        rounded = current.astype(jnp.bfloat16)
        group_block = lax.all_gather(rounded, "col", axis=0, tiled=True)
        per_column = row_count // col_count
        received = [
            broadcast(group_block, "row", col_index * per_column + member)
            for member in range(per_column)
        ]
        column_block = jnp.concatenate(received, axis=0)
        traces = jnp.dot(interp_block, group_block, preferred_element_type=jnp.float32).astype(
            jnp.bfloat16
        )
        segment = lax.all_gather(traces[None], "col", axis=0, tiled=True)
        owners = jnp.arange(segment.shape[0], dtype=jnp.int32)
        counts = jnp.sum((local_adjacent[None, :] == owners[:, None]).astype(jnp.float32), axis=1)
        neighbours = jnp.einsum(
            "p,pmn->mn", counts.astype(jnp.bfloat16), segment, preferred_element_type=jnp.float32
        )
        own_wide = traces.astype(jnp.float32)
        combined = jnp.dot(dtn_block, traces, preferred_element_type=jnp.float32) + own_wide
        combined = combined + face_weight * (NADJ * own_wide - neighbours)
        response = combined.astype(jnp.bfloat16)
        surface_part = jnp.dot(surface, column_block, preferred_element_type=jnp.float32)
        volume_part = lax.dot_general(
            interp_block, response, (((0,), (0,)), ((), ())), preferred_element_type=jnp.float32
        )
        summed = lax.psum_scatter(
            (surface_part + volume_part).astype(jnp.bfloat16),
            "col",
            scatter_dimension=0,
            tiled=True,
        ).astype(jnp.float32)
        residual = excitation - current - summed
        current = current + damping * residual
    return (current, residual)


def solution(mesh):
    in_specs = (
        P("row", "col"),
        P(("row", "col"), None),
        P(("row", "col"), None, None),
        P(("row", "col"), None, None),
        P(("row", "col"), None),
    )
    out_specs = (P(("row", "col"), None), P(("row", "col"), None))
    return jax.shard_map(local, mesh=mesh, in_specs=in_specs, out_specs=out_specs, check_vma=False)
```

profile of v0, /device:TPU:7, one launch (start us, length us, event | category | flops | bytes accessed | tf_op | source)
XLA Modules:
  0.0 247.4 jit_solution(15848962410064258992)
XLA Ops:
  8.0 0.0 copy-start
  8.0 0.0 all-reduce.7.cloned.1.call-start
  8.1 1.2 copy.18
  9.3 14.5 %all_gather.12 = bf16[2048,128]{0,1:T(8,128)(2,1)S(1)} all-gather(bf16[512,128]{0,1:T(8,128)(2,1)S(1)} %convert_element_type.58), channel_id=1, replica_groups=mesh['row'=8,'col'=4] {'col'}, dimensions={0}, use_global_device_ids=true | all-gather | bytes 655360 | tf_op jit(solution)/shard_map/all_gather | solution.py:30
  23.8 1.0 broadcast_select_fusion.3
  24.9 0.0 copy-start.2
  24.9 0.0 all-reduce.7.cloned.1.call-update
  24.9 0.0 all-gather.5.cloned.1.call-start
  24.9 4.1 %fusion.54 = bf16[1024,128]{1,0:T(8,128)(2,1)} fusion(bf16[2048,128]{0,1:T(8,128)(2,1)S(1)} %all_gather.12, bf16[1,1024,2048]{2,1,0:T(8,128)(2,1)} %param.8), kind=kOutput, calls=%fused_computation.26 | convolution fusion | flops 537001984 | bytes 4980736 | tf_op jit(solution)/shard_map/dot_general | solution.py:37
  29.1 0.0 all-gather.5.cloned.1.call-update
  29.1 0.0 reduce-scatter.3.cloned.1.call-start
  29.2 0.0 copy-done.2
  29.2 0.1 convert_reduce_fusion
  29.3 53.3 %all-reduce.7.cloned.1.call-done = (bf16[2048,128]{0,1:T(8,128)(2,1)}, bf16[2048,128]{0,1:T(8,128)(2,1)}) async-done(((bf16[2048,128]{0,1:T(8,128)(2,1)}, bf16[2048,128]{0,1:T(8,128)(2,1)}), (bf16[2048,128]{0,1:T(8,128)(2,1)}, bf16[2048,128]{0,1:T(8,128)(2,1)})) %all-reduce.7.cloned.1.call-update) | async-done | bytes 1048592 | tf_op jit(solution)/shard_map/psum | solution.py:16
  82.6 11.8 %fusion.60 = f32[128,2048]{1,0:T(8,128)S(1)} fusion(bf16[2048,4096]{1,0:T(8,128)(2,1)} %param.5, bf16[2048,128]{0,1:T(8,128)(2,1)} %get-tuple-element.8, bf16[2048,128]{0,1:T(8,128)(2,1)} %get-tuple-element.9), kind=kOutput, calls=%fused_computation.28 | convolution fusion | flops 2149580800 | bytes 18874368 | tf_op jit(solution)/shard_map/dot_general | solution.py:50
  94.4 0.0 all-gather.5.cloned.1.call-done
  94.4 3.0 %fusion.70 = f32[1,1024,128]{2,0,1:T(1,128)} fusion(bf16[4,1024,128]{2,1,0:T(8,128)(2,1)} %bitcast.101, bf16[4]{0:T(256)(128)(2,1)S(1)} %convert_reduce_fusion), kind=kOutput, calls=%fused_computation.38 | convolution fusion | flops 1048576 | bytes 1572872 | tf_op jit(solution)/shard_map/p,pmn->mn/dot_general | solution.py:43
  97.3 0.0 copy-done
  97.3 4.6 %fusion.20 = bf16[2048,128]{0,1:T(8,128)(2,1)} fusion(f32[128,2048]{1,0:T(8,128)S(1)} %fusion.60, bf16[1,1024,2048]{2,1,0:T(8,128)(2,1)} %param.8, bf16[1024,128]{1,0:T(8,128)(2,1)} %fusion.54, bf16[1,1024,1024]{2,1,0:T(8,128)(2,1)S(1)} %copy-done, f32[1024,128]{1,0:T(8,128)} %bitcast.100), kind=kOutput, calls=%fused_computation.12 | convolution fusion | flops 806748160 | bytes 8650752 | tf_op jit(solution)/shard_map/dot_general | solution.py:51
  101.9 0.0 reduce-scatter.3.cloned.1.call-update
  101.9 0.0 all-reduce.5.cloned.1.call-start
  102.0 21.8 %reduce-scatter.3.cloned.1.call-done = bf16[512,128]{0,1:T(8,128)(2,1)} async-done(((bf16[2048,128]{0,1:T(8,128)(2,1)}), bf16[512,128]{0,1:T(8,128)(2,1)}) %reduce-scatter.3.cloned.1.call-update) | async-done | bytes 131088 | tf_op jit(solution)/shard_map/reduce_scatter | solution.py:54
  123.8 1.0 fusion.88
  124.7 12.5 %all_gather.14 = bf16[2048,128]{0,1:T(8,128)(2,1)S(1)} all-gather(bf16[512,128]{0,1:T(8,128)(2,1)S(1)} %fusion.88), channel_id=1, replica_groups=mesh['row'=8,'col'=4] {'col'}, dimensions={0}, use_global_device_ids=true | all-gather | bytes 655360 | tf_op jit(solution)/shard_map/all_gather | solution.py:30
  137.2 1.0 broadcast_select_fusion.2
  138.3 0.0 all-reduce.5.cloned.1.call-update
  138.3 0.0 all-gather.7.cloned.1.call-start
  138.4 4.1 %fusion.57 = bf16[128,1024]{0,1:T(8,128)(2,1)} fusion(bf16[2048,128]{0,1:T(8,128)(2,1)S(1)} %all_gather.14, bf16[1,1024,2048]{2,1,0:T(8,128)(2,1)} %param.8), kind=kOutput, calls=%fused_computation.27 | convolution fusion | flops 537001984 | bytes 4980736 | tf_op jit(solution)/shard_map/dot_general | solution.py:37
  142.5 0.0 all-gather.7.cloned.1.call-update
  142.5 0.2 reduce-scatter.5.cloned.1.call-start
  142.8 53.1 %all-reduce.5.cloned.1.call-done = (bf16[2048,128]{0,1:T(8,128)(2,1)}, bf16[2048,128]{0,1:T(8,128)(2,1)}) async-done(((bf16[2048,128]{0,1:T(8,128)(2,1)}, bf16[2048,128]{0,1:T(8,128)(2,1)}), (bf16[2048,128]{0,1:T(8,128)(2,1)}, bf16[2048,128]{0,1:T(8,128)(2,1)})) %all-reduce.5.cloned.1.call-update) | async-done | bytes 1048592 | tf_op jit(solution)/shard_map/psum | solution.py:16
  195.9 11.8 %fusion.64 = f32[128,2048]{1,0:T(8,128)S(1)} fusion(bf16[2048,4096]{1,0:T(8,128)(2,1)} %param.5, bf16[2048,128]{0,1:T(8,128)(2,1)} %get-tuple-element.6, bf16[2048,128]{0,1:T(8,128)(2,1)} %get-tuple-element.7), kind=kOutput, calls=%fused_computation.32 | convolution fusion | flops 2149580800 | bytes 18874368 | tf_op jit(solution)/shard_map/dot_general | solution.py:50
  207.6 0.0 all-gather.7.cloned.1.call-done
  207.7 3.0 %fusion.68 = f32[1,1024,128]{2,0,1:T(1,128)} fusion(bf16[4,1024,128]{2,1,0:T(8,128)(2,1)} %bitcast.102, bf16[4]{0:T(256)(128)(2,1)S(1)} %convert_reduce_fusion), kind=kOutput, calls=%fused_computation.36 | convolution fusion | flops 1048576 | bytes 1572872 | tf_op jit(solution)/shard_map/p,pmn->mn/dot_general | solution.py:43
  210.6 0.0 copy-start.1
  210.6 4.6 %fusion.23 = bf16[2048,128]{0,1:T(8,128)(2,1)} fusion(f32[128,2048]{1,0:T(8,128)S(1)} %fusion.64, bf16[1,1024,2048]{2,1,0:T(8,128)(2,1)} %param.8, bf16[128,1024]{0,1:T(8,128)(2,1)} %fusion.57, bf16[1,1024,1024]{2,1,0:T(8,128)(2,1)S(1)} %copy-done, f32[1024,128]{1,0:T(8,128)} %bitcast.99), kind=kOutput, calls=%fused_computation.13 | convolution fusion | flops 806748160 | bytes 8650752 | tf_op jit(solution)/shard_map/dot_general | solution.py:51
  215.2 0.0 reduce-scatter.5.cloned.1.call-update
  215.3 21.8 %reduce-scatter.5.cloned.1.call-done = bf16[512,128]{0,1:T(8,128)(2,1)} async-done(((bf16[2048,128]{0,1:T(8,128)(2,1)}), bf16[512,128]{0,1:T(8,128)(2,1)}) %reduce-scatter.5.cloned.1.call-update) | async-done | bytes 131088 | tf_op jit(solution)/shard_map/reduce_scatter | solution.py:54
  237.1 0.0 copy-done.1
  237.1 1.0 convert_subtract_fusion
  238.1 0.8 copy.22
  238.9 0.8 copy.21
  (2 shorter events, 0.0 us)
Async XLA Ops:
  8.0 89.4 %copy-start = (bf16[1,1024,1024]{2,1,0:T(8,128)(2,1)S(1)}, bf16[1,1024,1024]{2,1,0:T(8,128)(2,1)}, u32[]{:S(2)}) copy-start(bf16[1,1024,1024]{2,1,0:T(8,128)(2,1)} %param.7) | copy-start | bytes 6291460
  8.0 74.6 %all-reduce.7.cloned.1.call-start = ((), (), s32[]{:S(2)}) async-start(), calls=%async_computation.7 | async-start | bytes 2097152 | tf_op jit(solution)/shard_map/psum | solution.py:16
  24.9 4.3 %copy-start.2 = (s32[1,6]{1,0:T(1,128)S(1)}, s32[1,6]{1,0:T(1,128)}, u32[]{:S(2)}) copy-start(s32[1,6]{1,0:T(1,128)} %param.9) | copy-start | bytes 76
  24.9 69.5 %all-gather.5.cloned.1.call-start = ((), (), s32[]{:S(2)}) async-start(), calls=%async_computation.4 | async-start | bytes 1310720 | tf_op jit(solution)/shard_map/all_gather | solution.py:40
  29.1 94.7 %reduce-scatter.3.cloned.1.call-start = ((), (), s32[]{:S(2)}) async-start(), calls=%async_computation.2 | async-start | bytes 655360 | tf_op jit(solution)/shard_map/reduce_scatter | solution.py:54
  101.9 93.9 %all-reduce.5.cloned.1.call-start = ((), (), s32[]{:S(2)}) async-start(), calls=%async_computation.6 | async-start | bytes 2097152 | tf_op jit(solution)/shard_map/psum | solution.py:16
  138.3 69.4 %all-gather.7.cloned.1.call-start = ((), (), s32[]{:S(2)}) async-start(), calls=%async_computation.5 | async-start | bytes 1310720 | tf_op jit(solution)/shard_map/all_gather | solution.py:40
  142.5 94.6 %reduce-scatter.5.cloned.1.call-start = ((), (), s32[]{:S(2)}) async-start(), calls=%async_computation.3 | async-start | bytes 655360 | tf_op jit(solution)/shard_map/reduce_scatter | solution.py:54
  210.6 26.5 %copy-start.1 = (bf16[512,128]{0,1:T(8,128)(2,1)S(1)}, bf16[512,128]{0,1:T(8,128)(2,1)}, u32[]{:S(2)}) copy-start(bf16[512,128]{0,1:T(8,128)(2,1)} %reduce-scatter.3.cloned.1.call-done) | copy-start | bytes 393220
Sparse Core Ops, SparseCore 0:
  25.0 57.5 all-reduce.6
  138.4 57.3 all-reduce.4
Sparse Core Ops, SparseCore 1:
  29.2 30.2 all-gather.4
  102.0 21.7 reduce-scatter.2
  142.6 30.1 all-gather.6
  215.3 21.7 reduce-scatter.4
where the time goes:
time: 251 us; the launch traced here: 247 us
  waiting for transfers between devices  150 us (60%)
  matrix products  46.9 us (19%)
  blocking collectives  27 us (11%)
  between operations  15.8 us (6%)
  other arithmetic  4.18 us (2%)
  local copies, waits for them, and re-layouts  2.9 us (1%)
    psum x2, waiting for transfers between devices, broadcast(): return lax.psum(kept, axis)  106 us
    reduce_scatter x2, waiting for transfers between devices, local(): lax.psum_scatter((surface_part + volume_part).astype(jnp.bfloat16), 'col'...  43.6 us
    all_gather x2, blocking collectives, local(): group_block = lax.all_gather(rounded, 'col', axis=0, tiled=True)  27 us
    dot_general x2, matrix products, local(): jnp.dot(surface, column_block, preferred_element_type=jnp.float32)  23.5 us
    dot_general x2, matrix products, local(): lax.dot_general(interp_block, response, (((0,), (0,)), ((), ())), preferr...  9.18 us
    dot_general x2, matrix products, local(): jnp.dot(interp_block, group_block, preferred_element_type=jnp.float32)  8.29 us
    dot_general x2, matrix products, local(): jnp.einsum('p,pmn->mn', counts.astype(jnp.bfloat16), segment, preferred_e...  5.92 us
  transfers between devices with their start and end apart: 6, of which 4 were waited for; matrix products, arithmetic and copies ran while one was open for 13% of the time, Pallas kernels for 0%

commit v1 on v0

v1 whole, which is shorter than its diff:
```python
import functools

import jax
import jax.numpy as jnp
from jax import lax
from jax.experimental import pallas as pl
from jax.experimental.pallas import tpu as pltpu
from jax.sharding import PartitionSpec as P

ITERS = 2
NADJ = 6

damping = 0.25
face_weight = 0.25
F32, BF16 = jnp.float32, jnp.bfloat16


def xor(a, b, bits):
    total = 0
    for i in range(bits):
        x, y = a // 2**i % 2, b // 2**i % 2
        total = total + (x + y - 2 * x * y) * 2**i
    return total


def gray(p, bits):
    return xor(p, p // 2, bits)


def ungray(g, bits):
    total, above = 0, 0
    for i in reversed(range(bits)):
        bit = g // 2**i % 2
        above = above + bit - 2 * above * bit
        total = total + above * 2**i
    return total


def kernel(
    R, n, tile,
    exc_hbm, interp_hbm, surf_hbm, dtn_hbm, adj,
    sol_ref, res_ref,
    exc, interp, surf, dtn, grp, colb, trc, acc, part, sbuf, rbuf,
    load_sem, g_ss, g_rs, t_ss, t_rs, c_ss, c_rs, p_ss, p_rs, r_ss, r_rs,
):
    half_n = n // 2
    bits = n.bit_length() - 1
    _, _, hs, ne = grp.shape[1:]
    m = interp.shape[0]
    rb = interp.shape[1]
    tiles = surf.shape[0] // tile
    r, c = lax.axis_index("row"), lax.axis_index("col")
    core, chip = r % 2, r // 2
    pos = ungray(xor(chip, c, bits), bits)
    right, left = (r, (c + 1) % n), (r, (c + n - 1) % n)
    partner = (chip * 2 + 1 - core, c)
    gnext = (xor(gray((pos + 1) % n, bits), c, bits) * 2 + core, c)
    gprev = (xor(gray((pos + n - 1) % n, bits), c, bits) * 2 + core, c)

    loads = [
        pltpu.make_async_copy(exc_hbm, exc, load_sem.at[0]),
        pltpu.make_async_copy(interp_hbm, interp, load_sem.at[1]),
    ]
    for i in range(tiles):
        rows = pl.ds(i * tile, tile)
        loads.append(pltpu.make_async_copy(surf_hbm.at[rows], surf.at[rows], load_sem.at[3 + i]))
    loads.append(pltpu.make_async_copy(dtn_hbm, dtn, load_sem.at[2]))
    for load in loads:
        load.start()

    barrier = pltpu.get_barrier_semaphore()
    for device in (left, right, partner, gnext, gprev):
        pl.semaphore_signal(barrier, inc=1, device_id=device, device_id_type=pl.DeviceIdType.MESH)
    pl.semaphore_wait(barrier, 5)

    def remote(src, dst, ss, rs, device):
        return pltpu.make_async_remote_copy(
            src_ref=src, dst_ref=dst, send_sem=ss, recv_sem=rs,
            device_id=device, device_id_type=pl.DeviceIdType.MESH,
        )

    def ring(buf, ss, rs, s, d, t, h, receive=False):
        hop = t if receive else t - 1
        owner = (c + n - hop) % n if d == 0 else (c + hop) % n
        block = buf.at[s, owner, h]
        return remote(block, block, ss.at[s, d, t - 1, h], rs.at[s, d, t - 1, h], right if d == 0 else left)

    def halves(d, t):
        if t == half_n:
            return (d,)
        return (d, 1 - d)

    waits = []

    def chain(s, owner, delta):
        def copies(src):
            out = []
            for h in range(2):
                block = src.at[owner, h]
                dst = colb.at[s, core, owner, h]
                k = (s, delta, h)
                out.append((
                    remote(block, dst, c_ss.at[k], c_rs.at[k], gnext if h == 0 else gprev),
                    remote(block, dst, p_ss.at[k], p_rs.at[k], partner),
                ))
            return out

        more = (pos != n - 1, pos != 1)

        @pl.when(pos == 0)
        def _():
            for h, (on, share) in enumerate(copies(grp.at[s])):
                on.start()
                share.start()

        @pl.when(pos != 0)
        def _():
            for h, (on, share) in enumerate(copies(colb.at[s, core])):
                on.wait_recv()

                @pl.when(more[h])
                def _():
                    on.start()

                share.start()

        for h, (on, share) in enumerate(copies(colb.at[s, core])):
            waits.append((more[h], on))
            waits.append((None, share))

    def chain_done(s, owner, delta):
        for h in range(2):
            block = colb.at[s, 1 - core, owner, h]
            k = (s, delta, h)
            remote(block, block, p_ss.at[k], p_rs.at[k], partner).wait_recv()

    counts = []
    for p in range(n):
        count = jnp.float32(0)
        for k in range(NADJ):
            count = count + jnp.where(adj[0, k] % n == p, 1.0, 0.0).astype(F32)
        counts.append(count)

    loads[0].wait()
    for s in range(ITERS):
        base = exc if s == 0 else sol_ref
        rounded = base[...].astype(BF16)
        grp[s, c] = rounded.reshape(2, hs, ne)

        for t in range(1, half_n + 1):
            for i in range(2):
                for d in range(2):
                    h = halves(d, t)
                    if i < len(h):
                        copy = ring(grp, g_ss, g_rs, s, d, t, h[i])
                        if t > 1:
                            ring(grp, g_ss, g_rs, s, d, t - 1, h[i], True).wait_recv()
                        copy.start()
                        waits.append((None, copy))
            if t > 1:
                for d in range(2):
                    for h in halves(d, t - 1):
                        if h not in halves(d, t):
                            ring(grp, g_ss, g_rs, s, d, t - 1, h, True).wait_recv()
            if t == 1:
                chain_order = [(c, 0)]
        for d in range(2):
            for h in halves(d, half_n):
                ring(grp, g_ss, g_rs, s, d, half_n, h, True).wait_recv()
        chain_order = [((c + k) % n, k) for k in range(n)]

        @pl.when(pos == 0)
        def _():
            colb[s, core] = grp[s]

        if s == 0:
            loads[1].wait()
        group = grp[s].reshape(rb, ne)
        for h in range(2):
            rows = pl.ds(h * (m // 2), m // 2)
            value = jnp.dot(interp[rows, :], group, preferred_element_type=F32)
            trc[s, c, h] = value.astype(BF16)
            for d in range(2):
                copy = ring(trc, t_ss, t_rs, s, d, 1, h)
                copy.start()
                waits.append((None, copy))

        def trace_step(t):
            for i in range(2):
                for d in range(2):
                    h = halves(d, t)
                    if i < len(h):
                        ring(trc, t_ss, t_rs, s, d, t - 1, h[i], True).wait_recv()
                        copy = ring(trc, t_ss, t_rs, s, d, t, h[i])
                        copy.start()
                        waits.append((None, copy))
            for d in range(2):
                for h in halves(d, t - 1):
                    if h not in halves(d, t):
                        ring(trc, t_ss, t_rs, s, d, t - 1, h, True).wait_recv()

        for k, (owner, delta) in enumerate(chain_order):
            chain(s, owner, delta)
            if k >= 1 and k + 1 <= half_n:
                trace_step(k + 1)
        for owner, delta in chain_order:
            chain_done(s, owner, delta)

        column = colb[s].reshape(2 * rb, ne)
        for i in range(tiles):
            if s == 0:
                loads[2 + i].wait()
            rows = pl.ds(i * tile, tile)
            acc[rows, :] = jnp.dot(surf[rows, :], column, preferred_element_type=F32)

        if s == 0:
            loads[-1].wait()
        own = trc[s, c].reshape(m, ne)
        combined = jnp.dot(dtn[...], own, preferred_element_type=F32)
        combined = combined + (1.0 + face_weight * NADJ) * own.astype(F32)
        for d in range(2):
            for h in halves(d, half_n):
                ring(trc, t_ss, t_rs, s, d, half_n, h, True).wait_recv()
        neighbours = counts[0] * trc[s, 0].reshape(m, ne).astype(F32)
        for p in range(1, n):
            neighbours = neighbours + counts[p] * trc[s, p].reshape(m, ne).astype(F32)
        response = combined - face_weight * neighbours
        turned = response.T.astype(BF16)
        volume = jnp.dot(turned, interp[...], preferred_element_type=F32)
        part[...] = (acc[...] + volume.T).reshape(n, 2, hs, ne)

        def summing(d, t, h):
            k = (s, d, t - 1, h)
            return remote(sbuf.at[k], rbuf.at[k], r_ss.at[k], r_rs.at[k], right if d == 0 else left)

        for t in range(half_n, 0, -1):
            for i in range(2):
                for d in range(2):
                    hh = halves(d, t)
                    if i < len(hh):
                        h = hh[i]
                        target = (c + t) % n if d == 0 else (c + n - t) % n
                        value = part[target, h]
                        if t < half_n and h in halves(d, t + 1):
                            summing(d, t + 1, h).wait_recv()
                            value = value + rbuf[s, d, t, h].astype(F32)
                        sbuf[s, d, t - 1, h] = value.astype(BF16)
                        copy = summing(d, t, h)
                        copy.start()
                        waits.append((None, copy))
        for h in range(2):
            rows = pl.ds(h * hs, hs)
            total = part[c, h]
            for d in range(2):
                summing(d, 1, h).wait_recv()
                total = total + rbuf[s, d, 0, h].astype(F32)
            current = base[rows, :]
            residual = exc[rows, :] - current - total
            res_ref[rows, :] = residual
            sol_ref[rows, :] = current + damping * residual

    for condition, copy in waits:
        if condition is None:
            copy.wait_send()
        else:
            pl.when(condition)(copy.wait_send)


def local(surface, excitation, dtn_blocks, interp_blocks, adjacency):
    R, n = lax.axis_size("row"), lax.axis_size("col")
    shard, ne = excitation.shape
    m, rb = interp_blocks.shape[1:]
    hs = shard // 2
    tile = min(512, surface.shape[0])
    assert R == 2 * n and n % 2 == 0 and n & (n - 1) == 0
    hops = n // 2
    vmem, hbm = pltpu.VMEM, pl.BlockSpec(memory_space=pl.ANY)
    dma = pltpu.SemaphoreType.DMA
    out = jax.ShapeDtypeStruct((shard, ne), F32)
    S = ITERS
    ring_sems = [dma((S, 2, hops, 2))] * 2
    chain_sems = [dma((S, n, 2))] * 2
    return pl.pallas_call(
        functools.partial(kernel, R, n, tile),
        out_shape=(out, out),
        in_specs=[hbm, hbm, hbm, hbm, pl.BlockSpec(memory_space=pltpu.SMEM)],
        out_specs=(pl.BlockSpec(memory_space=vmem),) * 2,
        scratch_shapes=[
            vmem((shard, ne), F32),
            vmem((m, rb), BF16),
            vmem(surface.shape, BF16),
            vmem((m, m), BF16),
            vmem((S, n, 2, hs, ne), BF16),
            vmem((S, 2, n, 2, hs, ne), BF16),
            vmem((S, n, 2, m // 2, ne), BF16),
            vmem((rb, ne), F32),
            vmem((n, 2, hs, ne), F32),
            vmem((S, 2, hops, 2, hs, ne), BF16),
            vmem((S, 2, hops, 2, hs, ne), BF16),
            dma((3 + surface.shape[0] // tile,)),
            *ring_sems, *ring_sems, *chain_sems, *chain_sems, *ring_sems,
        ],
        compiler_params=pltpu.CompilerParams(
            collective_id=0, has_side_effects=True, vmem_limit_bytes=60 * 2**20
        ),
    )(excitation, interp_blocks.reshape(m, rb), surface, dtn_blocks.reshape(m, m), adjacency)


def solution(mesh):
    in_specs = (
        P("row", "col"),
        P(("row", "col"), None),
        P(("row", "col"), None, None),
        P(("row", "col"), None, None),
        P(("row", "col"), None),
    )
    out_specs = (P(("row", "col"), None), P(("row", "col"), None))
    return jax.shard_map(local, mesh=mesh, in_specs=in_specs, out_specs=out_specs, check_vma=False)
```

time: 251 us -> 191 us (0.76); the launches traced: 247 us -> 191 us
  Pallas kernels: 0 us -> 187 us
  waiting for transfers between devices: 150 us -> 0 us
  matrix products: 46.9 us -> 0 us
  blocking collectives: 27 us -> 0 us
  between operations: 15.8 us -> 0.64 us
  other arithmetic: 4.18 us -> 0 us
    pallas_call x0 -> x1, Pallas kernels: none -> 187 us  [local(): pl.pallas_call(functools.partial(kernel, R, n, tile), out_shape=(out, out...]
    psum x2 -> x0, waiting for transfers between devices: 106 us -> none  [broadcast(): return lax.psum(kept, axis)]
    dot_general x8 -> x0, matrix products: 46.9 us -> none  [the longest x2 23.5 us: local(): jnp.dot(surface, column_block, preferred_element_type=jnp.float32)]
    reduce_scatter x2 -> x0, waiting for transfers between devices: 43.6 us -> none  [local(): lax.psum_scatter((surface_part + volume_part).astype(jnp.bfloat16), 'col'...]
    all_gather x2 -> x0, blocking collectives: 27 us -> none  [local(): group_block = lax.all_gather(rounded, 'col', axis=0, tiled=True)]
  transfers between devices with their start and end apart: 6 -> 0, of which waited for: 4 -> 0; matrix products, arithmetic and copies ran while one was open for 13% -> 0% of each run, Pallas kernels for 0% -> 0%
where the time goes in v1:
time: 191 us
  Pallas kernels  187 us (98%)
  local copies, waits for them, and re-layouts  3.34 us (2%)
    pallas_call x1, Pallas kernels, local(): pl.pallas_call(functools.partial(kernel, R, n, tile), out_shape=(out, out...  187 us

profile of v1, /device:TPU:7, one launch (start us, length us, event | category | flops | bytes accessed | tf_op | source)
XLA Modules:
  0.0 190.8 jit_solution(2739573445994992762)
XLA Ops:
  0.6 186.8 %shard_map.68 = (f32[512,128]{1,0:T(8,128)}, f32[512,128]{1,0:T(8,128)}) custom-call(f32[512,128]{1,0:T(8,128)} %exc_hbm.1, bf16[1024,2048]{1,0:T(8,128)(2,1)} %bitcast.2, bf16[2048,4096]{1,0:T(8,128)(2,1)} %surf_hbm.1, bf16[1024,1024]{1,0:T(8,128)(2,1)} %bitcast.3, s32[1,6]{1,0:T(1,128)} %adj.1), custom_call_target="tpu_custom_call" | custom-call | tf_op jit(solution)/shard_map/pallas_call | solution.py:283
  187.5 1.7 copy.9
  189.1 1.7 copy.10

commit v2 on v1

--- a/solution.py
+++ b/solution.py
@@ -92,41 +92,55 @@
 
     waits = []
 
-    def chain(s, owner, delta):
-        def copies(src):
-            out = []
-            for h in range(2):
-                block = src.at[owner, h]
-                dst = colb.at[s, core, owner, h]
-                k = (s, delta, h)
-                out.append((
-                    remote(block, dst, c_ss.at[k], c_rs.at[k], gnext if h == 0 else gprev),
-                    remote(block, dst, p_ss.at[k], p_rs.at[k], partner),
-                ))
-            return out
-
-        more = (pos != n - 1, pos != 1)
-
+    def chain_copies(src, s, owner, delta, h):
+        block = src.at[owner, h]
+        dst = colb.at[s, core, owner, h]
+        k = (s, delta, h)
+        return (
+            remote(block, dst, c_ss.at[k], c_rs.at[k], gnext if h == 0 else gprev),
+            remote(block, dst, p_ss.at[k], p_rs.at[k], partner),
+        )
+
+    def chain_source(s, deltas):
         @pl.when(pos == 0)
         def _():
-            for h, (on, share) in enumerate(copies(grp.at[s])):
-                on.start()
-                share.start()
-
-        @pl.when(pos != 0)
-        def _():
-            for h, (on, share) in enumerate(copies(colb.at[s, core])):
-                on.wait_recv()
-
-                @pl.when(more[h])
-                def _():
+            for delta in deltas:
+                for h in range(2):
+                    on, _ = chain_copies(grp.at[s], s, (c + delta) % n, delta, h)
                     on.start()
-
-                share.start()
-
-        for h, (on, share) in enumerate(copies(colb.at[s, core])):
-            waits.append((more[h], on))
-            waits.append((None, share))
+            for delta in deltas:
+                for h in range(2):
+                    _, share = chain_copies(grp.at[s], s, (c + delta) % n, delta, h)
+                    share.start()
+
+    arrival = [0] + sorted(range(1, n), key=lambda k: min(k, n - k))
+
+    def chain_relay(s, phase):
+        for q in range(1, n):
+            pieces = []
+            for k, delta in enumerate(arrival):
+                for h in range(2):
+                    hops = q if h == 0 else n - q
+                    own_phase = 2 if hops > 1 else (0 if k == 0 else 1)
+                    if own_phase == phase:
+                        pieces.append((k + hops, -hops, k, delta, h))
+            pieces.sort()
+
+            @pl.when(pos == q)
+            def _():
+                for _, _, _, delta, h in pieces:
+                    on, share = chain_copies(colb.at[s, core], s, (c + delta) % n, delta, h)
+                    on.wait_recv()
+                    if q != (n - 1 if h == 0 else 1):
+                        on.start()
+                    share.start()
+
+    def chain_sent(s):
+        for delta in range(n):
+            for h in range(2):
+                on, share = chain_copies(colb.at[s, core], s, (c + delta) % n, delta, h)
+                waits.append((pos != (n - 1 if h == 0 else 1), on))
+                waits.append((None, share))
 
     def chain_done(s, owner, delta):
         for h in range(2):
@@ -141,20 +155,28 @@
             count = count + jnp.where(adj[0, k] % n == p, 1.0, 0.0).astype(F32)
         counts.append(count)
 
+    def send_own(s, h, value):
+        grp[s, c, h] = value.astype(BF16)
+        for d in range(2):
+            copy = ring(grp, g_ss, g_rs, s, d, 1, h)
+            copy.start()
+            waits.append((None, copy))
+
     loads[0].wait()
     for s in range(ITERS):
         base = exc if s == 0 else sol_ref
-        rounded = base[...].astype(BF16)
-        grp[s, c] = rounded.reshape(2, hs, ne)
-
-        for t in range(1, half_n + 1):
+        if s == 0:
+            for h in range(2):
+                send_own(0, h, exc[pl.ds(h * hs, hs), :])
+        chain_source(s, arrival[:1])
+
+        for t in range(2, half_n + 1):
             for i in range(2):
                 for d in range(2):
                     h = halves(d, t)
                     if i < len(h):
                         copy = ring(grp, g_ss, g_rs, s, d, t, h[i])
-                        if t > 1:
-                            ring(grp, g_ss, g_rs, s, d, t - 1, h[i], True).wait_recv()
+                        ring(grp, g_ss, g_rs, s, d, t - 1, h[i], True).wait_recv()
                         copy.start()
                         waits.append((None, copy))
             if t > 1:
@@ -162,12 +184,11 @@
                     for h in halves(d, t - 1):
                         if h not in halves(d, t):
                             ring(grp, g_ss, g_rs, s, d, t - 1, h, True).wait_recv()
-            if t == 1:
-                chain_order = [(c, 0)]
         for d in range(2):
             for h in halves(d, half_n):
                 ring(grp, g_ss, g_rs, s, d, half_n, h, True).wait_recv()
-        chain_order = [((c + k) % n, k) for k in range(n)]
+        chain_source(s, arrival[1:])
+        chain_relay(s, 0)
 
         @pl.when(pos == 0)
         def _():
@@ -199,12 +220,13 @@
                     if h not in halves(d, t):
                         ring(trc, t_ss, t_rs, s, d, t - 1, h, True).wait_recv()
 
-        for k, (owner, delta) in enumerate(chain_order):
-            chain(s, owner, delta)
-            if k >= 1 and k + 1 <= half_n:
-                trace_step(k + 1)
-        for owner, delta in chain_order:
-            chain_done(s, owner, delta)
+        chain_relay(s, 1)
+        for t in range(2, half_n + 1):
+            trace_step(t)
+        chain_relay(s, 2)
+        for delta in range(n):
+            chain_done(s, (c + delta) % n, delta)
+        chain_sent(s)
 
         column = colb[s].reshape(2 * rb, ne)
         for i in range(tiles):
@@ -236,7 +258,7 @@
         for t in range(half_n, 0, -1):
             for i in range(2):
                 for d in range(2):
-                    hh = halves(d, t)
+                    hh = halves(d, t)[:: -1 if t == half_n - 1 else 1]
                     if i < len(hh):
                         h = hh[i]
                         target = (c + t) % n if d == 0 else (c + n - t) % n
@@ -256,8 +278,11 @@
                 total = total + rbuf[s, d, 0, h].astype(F32)
             current = base[rows, :]
             residual = exc[rows, :] - current - total
+            updated = current + damping * residual
+            if s + 1 < ITERS:
+                send_own(s + 1, h, updated)
             res_ref[rows, :] = residual
-            sol_ref[rows, :] = current + damping * residual
+            sol_ref[rows, :] = updated
 
     for condition, copy in waits:
         if condition is None:

time: 191 us -> 110 us (0.58)
  Pallas kernels: 187 us -> 104 us
    pallas_call x1, Pallas kernels: 187 us -> 104 us  [local(): pl.pallas_call(functools.partial(kernel, R, n, tile), out_shape=(out, out...]
where the time goes in v2:
time: 110 us; the launch traced here: 108 us
  Pallas kernels  104 us (95%)
  local copies, waits for them, and re-layouts  3.34 us (3%)
    pallas_call x1, Pallas kernels, local(): pl.pallas_call(functools.partial(kernel, R, n, tile), out_shape=(out, out...  104 us
    unnamed x2, local copies, waits for them, and re-layouts  3.34 us

profile of v2, /device:TPU:7, one launch (start us, length us, event | category | flops | bytes accessed | tf_op | source)
XLA Modules:
  0.0 108.0 jit_solution(14579126612862534791)
XLA Ops:
  0.6 104.0 %shard_map.68 = (f32[512,128]{1,0:T(8,128)}, f32[512,128]{1,0:T(8,128)}) custom-call(f32[512,128]{1,0:T(8,128)} %exc_hbm.1, bf16[1024,2048]{1,0:T(8,128)(2,1)} %bitcast.2, bf16[2048,4096]{1,0:T(8,128)(2,1)} %surf_hbm.1, bf16[1024,1024]{1,0:T(8,128)(2,1)} %bitcast.3, s32[1,6]{1,0:T(1,128)} %adj.1), custom_call_target="tpu_custom_call" | custom-call | tf_op jit(solution)/shard_map/pallas_call | solution.py:308
  104.7 1.7 %copy.9 = f32[512,128]{1,0:T(8,128)} copy(f32[512,128]{1,0:T(8,128)} %get-tuple-element.4) | data formatting | bytes 524288
  106.3 1.7 %copy.10 = f32[512,128]{1,0:T(8,128)} copy(f32[512,128]{1,0:T(8,128)} %get-tuple-element.5) | data formatting | bytes 524288
